TPU v7x, 32 devices: a whole 2x2x4 slice. The times are simulated.
32 devices in a mesh: groups: 2 (over y), batch: 8 (over z, x), heads: 2 (over core).
Axes of the slice: x: 2, y: 2, z: 4, core: 2. Of those that a mesh axis runs over, the one named last changes fastest.
Arguments:
- storage: bfloat16 [1, 4096, 4608], P(None, ('groups', 'batch', 'heads')), parts along dimension 1, may hold values from -6 to 6
- block_table: int32 [4096], P('groups'), parts along dimension 0, may hold values from 0 to 2047, as said below
- lengths: int32 [16], P(('groups', 'batch')), parts along dimension 0, may hold values from 4 to 2048
- query: bfloat16 [16, 4, 128, 576], P(('groups', 'batch'), None, 'heads'), parts along dimension 0, may hold values from -10 to 10
Outputs:
- context: bfloat16 [16, 4, 128, 512], P(('groups', 'batch'), None, 'heads'), parts along dimension 0
There are 2 independent parts, one for each index of `groups`. A program takes and returns all parts, laid end to end along the dimension named above; each array names one. Nothing has to cross between parts.
Inputs may be any that keep to these rules, and one draw needn't show every extreme that they name: `block_table`: the entries are a permutation of 0 to 2047; entry g names block g mod 256 of sequence g // 256. Storage device k of the batch+heads order, with k = 2 b + p, holds for every batch index j exactly 16 blocks of sequences j * 1 to (j + 1) - 1, all with block numbers from p * 128 to (p + 1) * 128 - 1, in no particular order.
All inputs are finite; a program needn't handle non-finite values.
Results may differ from a plain program's by a relative error of at most 0.0031.
Values may be sent and summed in bfloat16 or wider, within the bound.
A program may use at most 64 MiB of HBM per device.

v0:
```python
import math
import jax
import jax.numpy as jnp
from jax import lax
from jax.sharding import PartitionSpec as P

LATENT = 512
ROPE = 64
HEAD_NOPE = 128
SEQ_DEV = 1
MAXLEN = 2048
BLK = 8
QTOK = 4


def partial_softmax(query_rows, key_rows, first_place, limits, score_scale):
    scores = (
        jnp.einsum("src,stc->srt", query_rows, key_rows, preferred_element_type=jnp.float32)
        * score_scale
    )
    places = first_place + jnp.arange(key_rows.shape[1], dtype=jnp.int32)
    visible = places[None, None, :] <= limits[:, :, None]
    masked = jnp.where(visible, scores, -1e30)
    highest = jnp.max(masked, axis=2)
    raised = jnp.where(visible, jnp.exp(masked - highest[:, :, None]), 0.0)
    totals = jnp.sum(raised, axis=2)
    mixed = jnp.einsum(
        "srt,stc->src",
        raised.astype(jnp.bfloat16),
        key_rows[:, :, :LATENT],
        preferred_element_type=jnp.float32,
    )
    return (highest, totals, mixed)


def local(storage, block_table, lengths, query):
    batch_count = lax.axis_size("batch")
    head_groups = lax.axis_size("heads")
    my_batch = lax.axis_index("batch")
    my_half = lax.axis_index("heads")
    slot_count = storage.shape[1]
    per_peer = slot_count // batch_count
    block_count = MAXLEN // BLK
    half_blocks = block_count // head_groups
    width = LATENT + ROPE
    zero_index = jnp.zeros((), jnp.int32)
    table_grid = block_table.reshape(batch_count, head_groups, slot_count)
    own_table = lax.dynamic_slice(
        table_grid, (my_batch, my_half, zero_index), (1, 1, slot_count)
    ).reshape(slot_count)
    owner = own_table // block_count // SEQ_DEV
    owner_table = (owner[:, None] == jnp.arange(batch_count, dtype=jnp.int32)[None, :]).astype(
        jnp.int32
    )
    rank = jnp.sum(owner_table * (jnp.cumsum(owner_table, axis=0) - 1), axis=1)
    send_place = owner * per_peer + rank
    order = (
        jnp.zeros((slot_count,), jnp.int32)
        .at[send_place]
        .set(jnp.arange(slot_count, dtype=jnp.int32))
    )
    outgoing = jnp.take(storage, order, axis=1)
    received = lax.all_to_all(outgoing, "batch", split_axis=1, concat_axis=1, tiled=True)
    sender_table = lax.dynamic_slice(
        table_grid, (zero_index, my_half, zero_index), (batch_count, 1, slot_count)
    ).reshape(batch_count, slot_count)
    sequence_ids = sender_table // block_count
    arrivals = sequence_ids // SEQ_DEV == my_batch
    arrive_place = (
        jnp.arange(batch_count, dtype=jnp.int32)[:, None] * per_peer
        + jnp.cumsum(arrivals.astype(jnp.int32), axis=1)
        - 1
    )
    target = (
        (sequence_ids - my_batch * SEQ_DEV) * half_blocks
        + sender_table % block_count
        - my_half * half_blocks
    )
    target = jnp.where(arrivals, target, slot_count)
    source = (
        jnp.zeros((slot_count,), jnp.int32)
        .at[target.reshape(-1)]
        .set(arrive_place.reshape(-1), mode="drop")
    )
    serving = jnp.take(received, source, axis=1)
    half_length = half_blocks * BLK
    seq_count = query.shape[0]
    local_keys = serving[0].reshape(seq_count, half_length * width)
    score_scale = 1.0 / math.sqrt(HEAD_NOPE + ROPE)
    every_query = lax.all_gather(query, "heads", axis=2, tiled=True)
    all_heads = every_query.shape[2]
    row_count = QTOK * all_heads
    query_rows = every_query.reshape(seq_count, row_count, width)
    draft = jnp.arange(row_count, dtype=jnp.int32) // all_heads
    limits = lengths[:, None] - QTOK + draft[None, :]
    key_rows = local_keys.reshape(seq_count, half_length, width)
    highest, totals, mixed = partial_softmax(
        query_rows, key_rows, my_half * half_length, limits, score_scale
    )
    shaped = (
        highest.reshape(1, seq_count, QTOK, all_heads),
        totals.reshape(1, seq_count, QTOK, all_heads),
        mixed.reshape(1, seq_count, QTOK, all_heads, LATENT),
    )
    pieces = (
        lax.all_to_all(shaped[0], "heads", split_axis=3, concat_axis=0, tiled=True),
        lax.all_to_all(shaped[1], "heads", split_axis=3, concat_axis=0, tiled=True),
        lax.all_to_all(shaped[2], "heads", split_axis=3, concat_axis=0, tiled=True),
    )
    overall = jnp.max(pieces[0], axis=0)
    factor = jnp.exp(pieces[0] - overall[None])
    totals = jnp.sum(pieces[1] * factor, axis=0)
    mixed = jnp.sum(pieces[2] * factor[..., None], axis=0)
    context = (mixed / totals[..., None]).astype(jnp.bfloat16)
    return context


def solution(mesh):
    in_specs = (
        P(None, ("groups", "batch", "heads"), None),
        P("groups"),
        P(("groups", "batch")),
        P(("groups", "batch"), None, "heads", None),
    )
    out_specs = P(("groups", "batch"), None, "heads", None)
    return jax.shard_map(local, mesh=mesh, in_specs=in_specs, out_specs=out_specs, check_vma=False)
```

profile of v0, /device:TPU:0, one launch (start us, length us, event | category | flops | bytes accessed | tf_op | source)
XLA Modules:
  0.0 96.7 jit_solution(5310189866146171281)
XLA Ops:
  3.0 1.0 %scatter_custom_fusion = s32[128]{0:T(128)S(1)} fusion(s32[128]{0:T(128)S(1)} %fusion.14, s32[128]{0:T(128)S(1)} %iota.24, s32[]{:T(128)} %constant.113.clone.1), kind=kCustom, calls=%fused_computation.74 | custom fusion | bytes 516 | tf_op jit(solution)/shard_map/scatter | solution.py:60
  4.1 4.3 %scatter_custom_fusion.1 = s32[128]{0:T(128)S(1)} fusion(s32[1024]{0:T(1024)S(1)} %bitcast.119, s32[1024]{0:T(1024)S(1)} %add_bitcast_fusion, s32[]{:T(128)} %constant.113.clone.1), kind=kCustom, calls=%fused_computation.72 | custom fusion | bytes 516 | tf_op jit(solution)/shard_map/scatter | solution.py:83
  8.4 1.3 %gather_fusion = bf16[128,4608]{1,0:T(8,128)(2,1)S(1)} fusion(bf16[128,4608]{1,0:T(8,128)(2,1)S(1)} %bitcast.103, s32[1024]{0:T(1024)S(1)} %pad_clamp_fusion.1), kind=kCustom, calls=%fused_computation.clone | custom fusion | bytes 2359808 | tf_op jit(solution)/shard_map/jit(_take)/gather | solution.py:62
  9.9 1.8 %copy.20 = bf16[1,128,4608]{2,0,1:T(2,128)(2,1)S(1)} copy(bf16[1,128,4608]{2,1,0:T(8,128)(2,1)S(1)} %bitcast_select_fusion.1) | data formatting | bytes 2359296 | tf_op jit(solution)/shard_map/jit(_take)/select_n | solution.py:62
  12.2 8.8 %reduce.8 = bf16[128,4608]{1,0:T(8,128)(2,1)} reduce(bf16[128,1,4608]{2,1,0:T(2,128)(2,1)S(1)} %bitcast.105, bf16[]{:T(256)} %broadcast.454), dimensions={1}, to_apply=%bitcast.102.reduce_sub_computation | reduce | bytes 2359298
  21.0 2.7 %reshape.485 = bf16[8,2,36864]{2,1,0:T(2,128)(2,1)} reshape(bf16[128,4608]{1,0:T(8,128)(2,1)} %reduce.8) | data formatting | bytes 2359296
  23.8 7.4 %all-to-all-start = ((bf16[8,2,36864]{2,1,0:T(2,128)(2,1)}), bf16[8,2,36864]{2,1,0:T(2,128)(2,1)S(1)}, u32[]{:S(2)}, u32[]{:S(2)}) async-start(bf16[8,2,36864]{2,1,0:T(2,128)(2,1)} %reshape.485), calls=%async_computation | async-start | bytes 2359296 | tf_op jit(solution)/shard_map/all_to_all | solution.py:63
  31.9 2.6 %all_gather.3 = bf16[1,4,128,576]{3,2,1,0:T(8,128)(2,1)} all-gather(bf16[1,4,64,576]{3,2,1,0:T(8,128)(2,1)S(1)} %copy-done.3), channel_id=1, replica_groups=mesh['groups'=2,'batch'=8,'heads'=2] {'heads'}, dimensions={2}, use_global_device_ids=true | all-gather | bytes 884736 | tf_op jit(solution)/shard_map/all_gather | solution.py:90
  34.5 25.3 %all-to-all-done = bf16[8,2,36864]{2,1,0:T(2,128)(2,1)S(1)} async-done(((bf16[8,2,36864]{2,1,0:T(2,128)(2,1)}), bf16[8,2,36864]{2,1,0:T(2,128)(2,1)S(1)}, u32[]{:S(2)}, u32[]{:S(2)}) %all-to-all-start) | async-done | bytes 1179680 | tf_op jit(solution)/shard_map/all_to_all | solution.py:63
  59.8 3.6 %reshape.486 = bf16[128,1,4608]{2,1,0:T(2,128)(2,1)} reshape(bf16[8,2,36864]{2,1,0:T(2,128)(2,1)S(1)} %all-to-all-done) | data formatting | bytes 2359296
  63.3 1.8 %copy.19 = bf16[1,128,4608]{2,1,0:T(8,128)(2,1)S(1)} copy(bf16[1,128,4608]{2,0,1:T(2,128)(2,1)} %bitcast.106) | data formatting | bytes 2359296
  65.2 1.3 %gather_fusion.1 = bf16[128,4608]{1,0:T(8,128)(2,1)S(1)} fusion(bf16[128,4608]{1,0:T(8,128)(2,1)S(1)} %bitcast.104, s32[1024]{0:T(1024)S(1)} %pad_clamp_fusion), kind=kCustom, calls=%fused_computation.1.clone | custom fusion | bytes 2359808 | tf_op jit(solution)/shard_map/jit(_take)/gather | solution.py:85
  66.6 1.9 %reshape.428 = bf16[1024,576]{1,0:T(8,128)(2,1)} reshape(bf16[1,128,4608]{2,1,0:T(8,128)(2,1)S(1)} %bitcast_select_fusion) | data formatting | bytes 2359296 | tf_op jit(solution)/shard_map/reshape.5
  68.5 1.9 %reshape_reshape_squeeze.3 = bf16[1,1024,576]{2,1,0:T(8,128)(2,1)} reshape(bf16[1,128,4608]{2,1,0:T(8,128)(2,1)S(1)} %bitcast_select_fusion) | data formatting | bytes 2359296 | tf_op jit(solution)/shard_map/reshape;reshape;squeeze | solution.py:96
  70.4 2.5 %fusion = (f32[512]{0:T(512)S(1)}, f32[1024,512]{0,1:T(8,128)S(1)}) fusion(s32[1024]{0:T(1024)S(1)} %iota_add_fusion, s32[512]{0:T(512)S(1)} %fusion.10, bf16[1024,576]{1,0:T(8,128)(2,1)} %reshape.428, bf16[512,576]{1,0:T(8,128)(2,1)S(1)} %bitcast.112), kind=kOutput, calls=%fused_computation.6 | convolution fusion | flops 606076416 | bytes 3874816 | tf_op jit(solution)/shard_map/src,stc->srt/dot_general | solution.py:18
  72.9 1.6 %fusion.1 = (f32[512]{0:T(512)S(1)}, bf16[512,1024]{1,0:T(8,128)(2,1)}) fusion(f32[1024,512]{0,1:T(8,128)S(1)} %get-tuple-element.11, f32[512]{0:T(512)S(1)} %get-tuple-element.10, s32[1024]{0:T(1024)S(1)} %iota_add_fusion, s32[512]{0:T(512)S(1)} %fusion.10), kind=kLoop, calls=%fused_computation.8 | loop fusion | flops 3669504 | bytes 3155968 | tf_op jit(solution)/shard_map/reduce_sum | solution.py:26
  75.1 0.8 reduce.11
  76.1 3.7 %all_to_all.62 = f32[2,1,256]{2,1,0:T(1,128)S(1)} all-to-all(f32[2,1,256]{2,1,0:T(1,128)S(1)} %reshape.489), channel_id=1, replica_groups=mesh['groups'=2,'batch'=8,'heads'=2] {'heads'}, dimensions={0} | all-to-all | bytes 4096 | tf_op jit(solution)/shard_map/all_to_all | solution.py:107
  80.7 0.8 reduce.9
  81.6 3.7 %all_to_all.63 = f32[2,1,256]{2,1,0:T(1,128)S(1)} all-to-all(f32[2,1,256]{2,1,0:T(1,128)S(1)} %reshape.487), channel_id=1, replica_groups=mesh['groups'=2,'batch'=8,'heads'=2] {'heads'}, dimensions={0} | all-to-all | bytes 4096 | tf_op jit(solution)/shard_map/all_to_all | solution.py:106
  86.1 1.9 %convolution_bitcast_fusion = f32[1,1,4,128,512]{4,3,2,1,0:T(8,128)S(1)} fusion(bf16[4,128,1024]{2,1,0:T(8,128)(2,1)} %bitcast.111, bf16[1,1024,576]{2,1,0:T(8,128)(2,1)S(1)} %copy-done.1), kind=kOutput, calls=%fused_computation.7 | convolution fusion | flops 536870912 | bytes 3145728 | tf_op jit(solution)/shard_map/srt,stc->src/dot_general | solution.py:27
  88.1 1.7 %copy.12 = f32[1,1,4,128,512]{4,2,1,0,3:T(4,128)} copy(f32[1,1,4,128,512]{4,3,2,1,0:T(8,128)S(1)} %convolution_bitcast_fusion) | data formatting | bytes 2097152 | tf_op jit(solution)/shard_map/srt,stc->src/dot_general | solution.py:27
  89.7 3.6 %all-to-all-start.1 = ((f32[1,1,4,128,512]{4,2,1,0,3:T(4,128)}), f32[1,1,4,128,512]{4,2,1,0,3:T(4,128)S(1)}, u32[]{:S(2)}, u32[]{:S(2)}) async-start(f32[1,1,4,128,512]{4,2,1,0,3:T(4,128)} %copy.12), calls=%async_computation.1 | async-start | bytes 2097152 | tf_op jit(solution)/shard_map/all_to_all | solution.py:108
  93.4 2.0 %all-to-all-done.1 = f32[1,1,4,128,512]{4,2,1,0,3:T(4,128)S(1)} async-done(((f32[1,1,4,128,512]{4,2,1,0,3:T(4,128)}), f32[1,1,4,128,512]{4,2,1,0,3:T(4,128)S(1)}, u32[]{:S(2)}, u32[]{:S(2)}) %all-to-all-start.1) | async-done | bytes 1048608 | tf_op jit(solution)/shard_map/all_to_all | solution.py:108
  (44 shorter events, 7.9 us)
Async XLA Ops:
  0.0 8.4 %copy-start = (bf16[1,128,4608]{2,1,0:T(8,128)(2,1)S(1)}, bf16[1,128,4608]{2,1,0:T(8,128)(2,1)}, u32[]{:S(2)}) copy-start(bf16[1,128,4608]{2,1,0:T(8,128)(2,1)} %param.6) | copy-start | bytes 3538948
  23.8 8.1 %copy-start.3 = (bf16[1,4,64,576]{3,2,1,0:T(8,128)(2,1)S(1)}, bf16[1,4,64,576]{3,2,1,0:T(8,128)(2,1)}, u32[]{:S(2)}) copy-start(bf16[1,4,64,576]{3,2,1,0:T(8,128)(2,1)} %param.9) | copy-start | bytes 884740
  23.8 36.0 %all-to-all-start = ((bf16[8,2,36864]{2,1,0:T(2,128)(2,1)}), bf16[8,2,36864]{2,1,0:T(2,128)(2,1)S(1)}, u32[]{:S(2)}, u32[]{:S(2)}) async-start(bf16[8,2,36864]{2,1,0:T(2,128)(2,1)} %reshape.485), calls=%async_computation | async-start | bytes 2359296 | tf_op jit(solution)/shard_map/all_to_all | solution.py:63
  68.5 1.9 %copy-start.2 = (bf16[1,4,128,576]{3,2,1,0:T(8,128)(2,1)S(1)}, bf16[1,4,128,576]{3,2,1,0:T(8,128)(2,1)}, u32[]{:S(2)}) copy-start(bf16[1,4,128,576]{3,2,1,0:T(8,128)(2,1)} %all_gather.3) | copy-start | bytes 1769476
  72.9 13.3 %copy-start.1 = (bf16[1,1024,576]{2,1,0:T(8,128)(2,1)S(1)}, bf16[1,1024,576]{2,1,0:T(8,128)(2,1)}, u32[]{:S(2)}) copy-start(bf16[1,1024,576]{2,1,0:T(8,128)(2,1)} %reshape_reshape_squeeze.3) | copy-start | bytes 3538948
  89.7 5.7 %all-to-all-start.1 = ((f32[1,1,4,128,512]{4,2,1,0,3:T(4,128)}), f32[1,1,4,128,512]{4,2,1,0,3:T(4,128)S(1)}, u32[]{:S(2)}, u32[]{:S(2)}) async-start(f32[1,1,4,128,512]{4,2,1,0,3:T(4,128)} %copy.12), calls=%async_computation.1 | async-start | bytes 2097152 | tf_op jit(solution)/shard_map/all_to_all | solution.py:108
where the time goes:
time: 97.3 us; the launch traced here: 96.7 us
  waiting for transfers between devices  27.3 us (28%)
  local copies, waits for them, and re-layouts  25.7 us (26%)
  other arithmetic  17.4 us (18%)
  starting transfers between devices  11 us (11%)
  blocking collectives  9.98 us (10%)
  matrix products  4.39 us (5%)
    all_to_all x1, waiting for transfers between devices, local(): lax.all_to_all(outgoing, 'batch', split_axis=1, concat_axis=1, tiled=True)  25.3 us
    unnamed x3, other arithmetic  10.5 us
    unnamed x17, local copies, waits for them, and re-layouts  9.66 us
    all_to_all x1, starting transfers between devices, local(): lax.all_to_all(outgoing, 'batch', split_axis=1, concat_axis=1, tiled=True)  7.41 us
    scatter x1, local copies, waits for them, and re-layouts, local(): source = jnp.zeros((slot_count,), jnp.int32).at[target.reshape(-1)].set(a...  4.3 us
    all_to_all x1, blocking collectives, local(): lax.all_to_all(shaped[0], 'heads', split_axis=3, concat_axis=0, tiled=True)  3.7 us
    all_to_all x1, blocking collectives, local(): lax.all_to_all(shaped[1], 'heads', split_axis=3, concat_axis=0, tiled=True)  3.7 us
    all_to_all x1, starting transfers between devices, local(): lax.all_to_all(shaped[2], 'heads', split_axis=3, concat_axis=0, tiled=True)  3.58 us
  transfers between devices with their start and end apart: 2, of which 2 were waited for; matrix products, arithmetic and copies ran while one was open for 0% of the time, Pallas kernels for 0%

commit v1 on v0

--- a/solution.py
+++ b/solution.py
@@ -60,7 +60,12 @@
         .set(jnp.arange(slot_count, dtype=jnp.int32))
     )
     outgoing = jnp.take(storage, order, axis=1)
-    received = lax.all_to_all(outgoing, "batch", split_axis=1, concat_axis=1, tiled=True)
+    received = jnp.concatenate(
+        lax.all_to_all(
+            jnp.stack(jnp.split(outgoing, lax.axis_size("batch"), axis=1)), "batch", 0, 0
+        ),
+        axis=1,
+    )
     sender_table = lax.dynamic_slice(
         table_grid, (zero_index, my_half, zero_index), (batch_count, 1, slot_count)
     ).reshape(batch_count, slot_count)

time: 97.3 us -> 77.8 us (0.80)
  other arithmetic: 17.4 us -> 7.9 us
  local copies, waits for them, and re-layouts: 25.7 us -> 20.6 us
  waiting for transfers between devices: 27.3 us -> 22.7 us
    unnamed x3 -> x2, other arithmetic: 10.5 us -> 1.61 us
    all_to_all x1, waiting for transfers between devices: 25.3 us -> 20.7 us  [local(): lax.all_to_all(jnp.stack(jnp.split(outgoing, lax.axis_size('batch'), axis...]
    unnamed x17 -> x22, local copies, waits for them, and re-layouts: 9.66 us -> 5.69 us
    select_n x1 -> x0, local copies, waits for them, and re-layouts: 1.82 us -> none  [local(): outgoing = jnp.take(storage, order, axis=1)]
    another operation x1 -> x2, local copies, waits for them, and re-layouts: 1.9 us -> 2.56 us
  transfers between devices with their start and end apart: 2 -> 2, of which waited for: 2 -> 2; matrix products, arithmetic and copies ran while one was open for 0% -> 6% of each run, Pallas kernels for 0% -> 0%
where the time goes in v1:
time: 77.8 us; the launch traced here: 77.3 us
  waiting for transfers between devices  22.7 us (29%)
  local copies, waits for them, and re-layouts  20.6 us (26%)
  starting transfers between devices  11 us (14%)
  blocking collectives  9.8 us (13%)
  other arithmetic  7.9 us (10%)
  matrix products  4.38 us (6%)
  between operations  0.92 us (1%)
    all_to_all x1, waiting for transfers between devices, local(): lax.all_to_all(jnp.stack(jnp.split(outgoing, lax.axis_size('batch'), axis...  20.7 us
    all_to_all x1, starting transfers between devices, local(): lax.all_to_all(jnp.stack(jnp.split(outgoing, lax.axis_size('batch'), axis...  7.41 us
    unnamed x22, local copies, waits for them, and re-layouts  5.69 us
    scatter x1, local copies, waits for them, and re-layouts, local(): source = jnp.zeros((slot_count,), jnp.int32).at[target.reshape(-1)].set(a...  4.3 us
    all_to_all x1, blocking collectives, local(): lax.all_to_all(shaped[1], 'heads', split_axis=3, concat_axis=0, tiled=True)  3.7 us
    all_to_all x1, blocking collectives, local(): lax.all_to_all(shaped[0], 'heads', split_axis=3, concat_axis=0, tiled=True)  3.7 us
    all_to_all x1, starting transfers between devices, local(): lax.all_to_all(shaped[2], 'heads', split_axis=3, concat_axis=0, tiled=True)  3.58 us
    dot_general x1, matrix products, partial_softmax(): jnp.einsum('src,stc->srt', query_rows, key_rows, preferred_element_type=j...  2.45 us
  transfers between devices with their start and end apart: 2, of which 2 were waited for; matrix products, arithmetic and copies ran while one was open for 6% of the time, Pallas kernels for 0%

profile of v1, /device:TPU:0, one launch (start us, length us, event | category | flops | bytes accessed | tf_op | source)
XLA Modules:
  0.0 77.3 jit_solution(16678191850732633052)
XLA Ops:
  0.0 0.8 %and_select_fusion.2 = s32[128]{0:T(128)S(1)} fusion(s32[8,2,128]{2,1,0:T(2,128)} %bitcast.146, s32[]{:T(128)S(6)} %select_n.126, s32[]{:T(128)S(6)} %select_n.127), kind=kLoop, calls=%fused_computation.72 | loop fusion | flops 1920 | bytes 1032 | tf_op jit(solution)/shard_map/jit(floor_divide)/jit(_where)/select_n | solution.py:51
  1.2 0.7 fusion.22
  1.9 1.0 %scatter_custom_fusion = s32[128]{0:T(128)S(1)} fusion(s32[128]{0:T(128)S(1)} %fusion.22, s32[128]{0:T(128)S(1)} %iota.24, s32[]{:T(128)} %constant.113.clone.1), kind=kCustom, calls=%fused_computation.89 | custom fusion | bytes 516 | tf_op jit(solution)/shard_map/scatter | solution.py:60
  3.0 1.3 %gather_fusion = bf16[128,4608]{1,0:T(8,128)(2,1)S(1)} fusion(bf16[128,4608]{1,0:T(8,128)(2,1)S(1)} %bitcast.131, s32[1024]{0:T(1024)S(1)} %pad_clamp_fusion.1), kind=kCustom, calls=%fused_computation.clone | custom fusion | bytes 2359808 | tf_op jit(solution)/shard_map/jit(_take)/gather | solution.py:62
  5.7 0.7 fusion.9
  8.4 0.7 fusion.5
  9.8 7.4 %all-to-all-start = ((bf16[8,1,16,4608]{3,2,1,0:T(8,128)(2,1)}), bf16[8,1,16,4608]{3,2,1,0:T(8,128)(2,1)S(1)}, u32[]{:S(2)}, u32[]{:S(2)}) async-start(bf16[8,1,16,4608]{3,2,1,0:T(8,128)(2,1)} %fusion.4), calls=%async_computation | async-start | bytes 2359296 | tf_op jit(solution)/shard_map/all_to_all | solution.py:64
  18.3 4.3 %scatter_custom_fusion.1 = s32[128]{0:T(128)S(1)} fusion(s32[1024]{0:T(1024)S(1)} %bitcast.145, s32[1024]{0:T(1024)S(1)} %add_bitcast_fusion, s32[]{:T(128)} %constant.113.clone.1), kind=kCustom, calls=%fused_computation.87 | custom fusion | bytes 516 | tf_op jit(solution)/shard_map/scatter | solution.py:88
  22.6 2.4 %all_gather.3 = bf16[1,4,128,576]{3,2,1,0:T(8,128)(2,1)} all-gather(bf16[1,4,64,576]{3,2,1,0:T(8,128)(2,1)S(1)} %copy-done.3), channel_id=1, replica_groups=mesh['groups'=2,'batch'=8,'heads'=2] {'heads'}, dimensions={2}, use_global_device_ids=true | all-gather | bytes 884736 | tf_op jit(solution)/shard_map/all_gather | solution.py:95
  25.1 20.7 %all-to-all-done = bf16[8,1,16,4608]{3,2,1,0:T(8,128)(2,1)S(1)} async-done(((bf16[8,1,16,4608]{3,2,1,0:T(8,128)(2,1)}), bf16[8,1,16,4608]{3,2,1,0:T(8,128)(2,1)S(1)}, u32[]{:S(2)}, u32[]{:S(2)}) %all-to-all-start) | async-done | bytes 1179680 | tf_op jit(solution)/shard_map/all_to_all | solution.py:64
  45.7 1.3 %gather_fusion.1 = bf16[128,4608]{1,0:T(8,128)(2,1)S(1)} fusion(bf16[128,4608]{1,0:T(8,128)(2,1)S(1)} %bitcast.132, s32[1024]{0:T(1024)S(1)} %pad_clamp_fusion), kind=kCustom, calls=%fused_computation.1.clone | custom fusion | bytes 2359808 | tf_op jit(solution)/shard_map/jit(_take)/gather | solution.py:90
  47.2 1.9 %reshape.432 = bf16[1024,576]{1,0:T(8,128)(2,1)} reshape(bf16[1,128,4608]{2,1,0:T(8,128)(2,1)S(1)} %bitcast_select_fusion) | data formatting | bytes 2359296 | tf_op jit(solution)/shard_map/reshape.5
  49.1 1.9 %reshape_reshape_squeeze.3 = bf16[1,1024,576]{2,1,0:T(8,128)(2,1)} reshape(bf16[1,128,4608]{2,1,0:T(8,128)(2,1)S(1)} %bitcast_select_fusion) | data formatting | bytes 2359296 | tf_op jit(solution)/shard_map/reshape;reshape;squeeze | solution.py:101
  51.0 2.5 %fusion = (f32[512]{0:T(512)S(1)}, f32[1024,512]{0,1:T(8,128)S(1)}) fusion(s32[1024]{0:T(1024)S(1)} %iota_add_fusion, s32[512]{0:T(512)S(1)} %fusion.18, bf16[1024,576]{1,0:T(8,128)(2,1)} %reshape.432, bf16[512,576]{1,0:T(8,128)(2,1)S(1)} %bitcast.138), kind=kOutput, calls=%fused_computation.6 | convolution fusion | flops 606076416 | bytes 3874816 | tf_op jit(solution)/shard_map/src,stc->srt/dot_general | solution.py:18
  53.4 1.6 %fusion.1 = (f32[512]{0:T(512)S(1)}, bf16[512,1024]{1,0:T(8,128)(2,1)}) fusion(f32[1024,512]{0,1:T(8,128)S(1)} %get-tuple-element.11, f32[512]{0:T(512)S(1)} %get-tuple-element.10, s32[1024]{0:T(1024)S(1)} %iota_add_fusion, s32[512]{0:T(512)S(1)} %fusion.18), kind=kLoop, calls=%fused_computation.8 | loop fusion | flops 3669504 | bytes 3155968 | tf_op jit(solution)/shard_map/reduce_sum | solution.py:26
  55.7 0.8 %reduce.10 = f32[128,4]{1,0:T(8,128)S(1)} reduce(f32[128,1,1,4]{3,2,1,0:T(1,128)S(1)} %bitcast.140, f32[]{:T(128)} %broadcast.454), dimensions={1,2}, to_apply=%bitcast.126.reduce_sub_computation | reduce | bytes 4100
  56.6 3.7 %all_to_all.62 = f32[2,1,256]{2,1,0:T(1,128)S(1)} all-to-all(f32[2,1,256]{2,1,0:T(1,128)S(1)} %reshape.491), channel_id=1, replica_groups=mesh['groups'=2,'batch'=8,'heads'=2] {'heads'}, dimensions={0} | all-to-all | bytes 4096 | tf_op jit(solution)/shard_map/all_to_all | solution.py:112
  61.3 0.8 %reduce.8 = f32[128,4]{1,0:T(8,128)S(1)} reduce(f32[128,1,1,4]{3,2,1,0:T(1,128)S(1)} %bitcast.141, f32[]{:T(128)} %broadcast.454), dimensions={1,2}, to_apply=%bitcast.124.reduce_sub_computation | reduce | bytes 4100
  62.2 3.7 %all_to_all.63 = f32[2,1,256]{2,1,0:T(1,128)S(1)} all-to-all(f32[2,1,256]{2,1,0:T(1,128)S(1)} %reshape.489), channel_id=1, replica_groups=mesh['groups'=2,'batch'=8,'heads'=2] {'heads'}, dimensions={0} | all-to-all | bytes 4096 | tf_op jit(solution)/shard_map/all_to_all | solution.py:111
  66.7 1.9 %convolution_bitcast_fusion = f32[1,1,4,128,512]{4,3,2,1,0:T(8,128)S(1)} fusion(bf16[4,128,1024]{2,1,0:T(8,128)(2,1)} %bitcast.137, bf16[1,1024,576]{2,1,0:T(8,128)(2,1)S(1)} %copy-done.1), kind=kOutput, calls=%fused_computation.7 | convolution fusion | flops 536870912 | bytes 3145728 | tf_op jit(solution)/shard_map/srt,stc->src/dot_general | solution.py:27
  68.6 1.7 %copy.9 = f32[1,1,4,128,512]{4,2,1,0,3:T(4,128)} copy(f32[1,1,4,128,512]{4,3,2,1,0:T(8,128)S(1)} %convolution_bitcast_fusion) | data formatting | bytes 2097152 | tf_op jit(solution)/shard_map/srt,stc->src/dot_general | solution.py:27
  70.3 3.6 %all-to-all-start.1 = ((f32[1,1,4,128,512]{4,2,1,0,3:T(4,128)}), f32[1,1,4,128,512]{4,2,1,0,3:T(4,128)S(1)}, u32[]{:S(2)}, u32[]{:S(2)}) async-start(f32[1,1,4,128,512]{4,2,1,0,3:T(4,128)} %copy.9), calls=%async_computation.1 | async-start | bytes 2097152 | tf_op jit(solution)/shard_map/all_to_all | solution.py:113
  74.0 2.0 %all-to-all-done.1 = f32[1,1,4,128,512]{4,2,1,0,3:T(4,128)S(1)} async-done(((f32[1,1,4,128,512]{4,2,1,0,3:T(4,128)}), f32[1,1,4,128,512]{4,2,1,0,3:T(4,128)S(1)}, u32[]{:S(2)}, u32[]{:S(2)}) %all-to-all-start.1) | async-done | bytes 1048608 | tf_op jit(solution)/shard_map/all_to_all | solution.py:113
  76.5 0.7 copy.12
  (49 shorter events, 8.4 us)
Async XLA Ops:
  0.0 3.0 %copy-start = (bf16[1,128,4608]{2,1,0:T(8,128)(2,1)S(1)}, bf16[1,128,4608]{2,1,0:T(8,128)(2,1)}, u32[]{:S(2)}) copy-start(bf16[1,128,4608]{2,1,0:T(8,128)(2,1)} %param.6) | copy-start | bytes 3538948
  9.7 7.4 %copy-start.4 = (s32[2048]{0:T(1024)S(1)}, s32[2048]{0:T(1024)}, u32[]{:S(2)}) copy-start(s32[2048]{0:T(1024)} %param.7) | copy-start | bytes 24580
  9.7 12.9 %copy-start.3 = (bf16[1,4,64,576]{3,2,1,0:T(8,128)(2,1)S(1)}, bf16[1,4,64,576]{3,2,1,0:T(8,128)(2,1)}, u32[]{:S(2)}) copy-start(bf16[1,4,64,576]{3,2,1,0:T(8,128)(2,1)} %param.9) | copy-start | bytes 884740
  9.8 36.0 %all-to-all-start = ((bf16[8,1,16,4608]{3,2,1,0:T(8,128)(2,1)}), bf16[8,1,16,4608]{3,2,1,0:T(8,128)(2,1)S(1)}, u32[]{:S(2)}, u32[]{:S(2)}) async-start(bf16[8,1,16,4608]{3,2,1,0:T(8,128)(2,1)} %fusion.4), calls=%async_computation | async-start | bytes 2359296 | tf_op jit(solution)/shard_map/all_to_all | solution.py:64
  49.1 1.9 %copy-start.2 = (bf16[1,4,128,576]{3,2,1,0:T(8,128)(2,1)S(1)}, bf16[1,4,128,576]{3,2,1,0:T(8,128)(2,1)}, u32[]{:S(2)}) copy-start(bf16[1,4,128,576]{3,2,1,0:T(8,128)(2,1)} %all_gather.3) | copy-start | bytes 1769476
  53.4 13.3 %copy-start.1 = (bf16[1,1024,576]{2,1,0:T(8,128)(2,1)S(1)}, bf16[1,1024,576]{2,1,0:T(8,128)(2,1)}, u32[]{:S(2)}) copy-start(bf16[1,1024,576]{2,1,0:T(8,128)(2,1)} %reshape_reshape_squeeze.3) | copy-start | bytes 3538948
  70.3 5.7 %all-to-all-start.1 = ((f32[1,1,4,128,512]{4,2,1,0,3:T(4,128)}), f32[1,1,4,128,512]{4,2,1,0,3:T(4,128)S(1)}, u32[]{:S(2)}, u32[]{:S(2)}) async-start(f32[1,1,4,128,512]{4,2,1,0,3:T(4,128)} %copy.9), calls=%async_computation.1 | async-start | bytes 2097152 | tf_op jit(solution)/shard_map/all_to_all | solution.py:113
